TPU v7x, 256 devices: a whole 4x4x8 slice. The times are simulated.
256 devices in a mesh: head: 8 (over x, core), seq: 32 (over y, z).
Axes of the slice: x: 4, y: 4, z: 8, core: 2. Of those that a mesh axis runs over, the one named last changes fastest.
Arguments:
- queries: bfloat16 [49152, 4096], P('seq', 'head'), may hold values from -32 to 32
- key_rows: bfloat16 [49152, 4096], P('seq', 'head'), may hold values from -32 to 32
- value_rows: bfloat16 [49152, 4096], P('seq', 'head'), may hold values from -6 to 6
- learn_rates: bfloat16 [49152, 8], P('seq', 'head'), may hold values from 0.00012683868 to 0.0012741089
- gate_fast: float32 [8, 512, 512], P('head'), may hold values from -0.25 to 0.25
- down_fast: float32 [8, 512, 512], P('head'), may hold values from -0.25 to 0.25
- up_fast: float32 [8, 512, 512], P('head'), may hold values from -0.25 to 0.25
Outputs:
- mixed: bfloat16 [49152, 4096], P('seq', 'head')
All inputs are finite; a program needn't handle non-finite values.
Results may differ from a plain program's by a relative error of at most 0.024.
Values may be sent and summed in bfloat16 or wider, within the bound.
A program may use at most 128 MiB of HBM per device.

v0:
```python
import math

import jax
import jax.numpy as jnp
from jax import lax
from jax.sharding import PartitionSpec as P

AH = 128
WINDOW = 512


EPSILON = 1e-06


def shifted(block, axis, distance):
    devices = range(lax.axis_size(axis))
    route = [(i - distance, i) for i in devices if i - distance in devices]
    return lax.ppermute(block, axis, route)


def norm_rows(values_in, heads_local, head_width):
    as_float = values_in.reshape(values_in.shape[0], heads_local, head_width).astype(jnp.float32)
    return (
        as_float / jnp.sqrt(jnp.mean(as_float * as_float, axis=-1, keepdims=True) + EPSILON)
    ).astype(jnp.bfloat16)


def fast_terms(fast_bf, key_norm, value_heads, rate_rows):
    gate_w, down_w, up_w = fast_bf
    gate_pre = jnp.einsum("nhd,hdf->nhf", key_norm, gate_w, preferred_element_type=jnp.float32)
    up_pre = jnp.einsum("nhd,hdf->nhf", key_norm, up_w, preferred_element_type=jnp.float32)
    sigmoid_gate = jax.nn.sigmoid(gate_pre)
    gate_act = gate_pre * sigmoid_gate
    hidden = (gate_act * up_pre).astype(jnp.bfloat16)
    scaled_val = (
        rate_rows.astype(jnp.float32)[:, :, None] * value_heads.astype(jnp.float32)
    ).astype(jnp.bfloat16)
    hidden_grad = -jnp.einsum(
        "nhe,hfe->nhf", scaled_val, down_w, preferred_element_type=jnp.float32
    )
    gate_grad = (
        hidden_grad * up_pre * sigmoid_gate * (1.0 + gate_pre * (1.0 - sigmoid_gate))
    ).astype(jnp.bfloat16)
    up_grad = (hidden_grad * gate_act).astype(jnp.bfloat16)
    gate_term = jnp.einsum("nhd,nhf->hdf", key_norm, gate_grad, preferred_element_type=jnp.float32)
    down_term = -jnp.einsum("nhf,nhe->hfe", hidden, scaled_val, preferred_element_type=jnp.float32)
    up_term = jnp.einsum("nhd,nhf->hdf", key_norm, up_grad, preferred_element_type=jnp.float32)
    return (gate_term, down_term, up_term)


def rescale(weight, moved):
    target_norm = jnp.sqrt(jnp.sum(weight * weight, axis=-2, keepdims=True))
    return moved * target_norm / jnp.sqrt(jnp.sum(moved * moved, axis=-2, keepdims=True) + EPSILON)


def apply_fast(fast_bf, query_norm):
    gate_w, down_w, up_w = fast_bf
    gate_pre = jnp.einsum("nhd,hdf->nhf", query_norm, gate_w, preferred_element_type=jnp.float32)
    up_pre = jnp.einsum("nhd,hdf->nhf", query_norm, up_w, preferred_element_type=jnp.float32)
    hidden = (gate_pre * jax.nn.sigmoid(gate_pre) * up_pre).astype(jnp.bfloat16)
    return jnp.einsum("nhf,hfe->nhe", hidden, down_w, preferred_element_type=jnp.float32).astype(
        jnp.bfloat16
    )


def renew(fast_f32, grad_terms):
    grad_sums = (
        lax.psum(grad_terms[0].astype(jnp.bfloat16), "seq").astype(jnp.float32),
        lax.psum(grad_terms[1].astype(jnp.bfloat16), "seq").astype(jnp.float32),
        lax.psum(grad_terms[2].astype(jnp.bfloat16), "seq").astype(jnp.float32),
    )
    renewed = tuple(
        (rescale(weight, weight - summed) for weight, summed in zip(fast_f32, grad_sums))
    )
    renewed_bf = tuple((weight.astype(jnp.bfloat16) for weight in renewed))
    return (renewed, renewed_bf)


def on_device(queries, key_rows, value_rows, learn_rates, gate_fast, down_fast, up_fast):
    heads_local = gate_fast.shape[0]
    head_width = gate_fast.shape[1]
    seq_count = lax.axis_size("seq")
    seq_index = lax.axis_index("seq")
    rows_here = queries.shape[0]
    width_here = queries.shape[1]
    fast_f32 = (gate_fast, down_fast, up_fast)
    first_bf = tuple((weight.astype(jnp.bfloat16) for weight in fast_f32))
    own_group = (seq_index >= seq_count // 2).astype(jnp.int32)
    query_norm = norm_rows(queries, heads_local, head_width)
    key_norm = norm_rows(key_rows, heads_local, head_width)
    value_heads = value_rows.reshape(rows_here, heads_local, head_width)
    fast_bf = first_bf
    kept = []
    for group in range(2):
        group_rates = jnp.where(own_group == group, learn_rates, jnp.zeros_like(learn_rates))
        grad_terms = fast_terms(fast_bf, key_norm, value_heads, group_rates)
        fast_f32, fast_bf = renew(fast_f32, grad_terms)
        kept.append(fast_bf)
    chosen = tuple(
        (jnp.where(own_group == 0, early, later) for early, later in zip(kept[0], kept[1]))
    )
    fast_out = apply_fast(chosen, query_norm).reshape(rows_here, width_here)
    attn_heads = width_here // AH
    score_scale = 1.0 / math.sqrt(AH)
    prev_keys, prev_values = shifted(
        (key_rows[rows_here - WINDOW :], value_rows[rows_here - WINDOW :]), "seq", 1
    )
    wide_keys = jnp.concatenate([prev_keys, key_rows], axis=0)
    wide_values = jnp.concatenate([prev_values, value_rows], axis=0)
    query_offset = jnp.arange(WINDOW, dtype=jnp.int32)[:, None]
    key_offset = jnp.arange(2 * WINDOW, dtype=jnp.int32)[None, :]
    block_outs = []
    for block in range(rows_here // WINDOW):
        lower = block * WINDOW
        start = seq_index * rows_here + lower
        query_block = queries[lower : lower + WINDOW].reshape(WINDOW, attn_heads, AH)
        key_block = wide_keys[lower : lower + 2 * WINDOW].reshape(2 * WINDOW, attn_heads, AH)
        value_block = wide_values[lower : lower + 2 * WINDOW].reshape(2 * WINDOW, attn_heads, AH)
        scores = (
            jnp.einsum("qhd,khd->hqk", query_block, key_block, preferred_element_type=jnp.float32)
            * score_scale
        )
        query_pos = start + query_offset
        key_pos = start - WINDOW + key_offset
        allowed = (key_pos <= query_pos) & (key_pos > query_pos - WINDOW) & (key_pos >= 0)
        scores = jnp.where(allowed[None], scores, jnp.float32(-1e30))
        top_score = jnp.max(scores, axis=-1, keepdims=True)
        expo = jnp.exp(scores - top_score)
        attend = (expo / jnp.sum(expo, axis=-1, keepdims=True)).astype(jnp.bfloat16)
        block_outs.append(
            jnp.einsum(
                "hqk,khd->qhd", attend, value_block, preferred_element_type=jnp.float32
            ).reshape(WINDOW, width_here)
        )
    attended = jnp.concatenate(block_outs, axis=0)
    return (fast_out.astype(jnp.float32) + attended).astype(jnp.bfloat16)


def solution(mesh):
    return jax.shard_map(
        on_device,
        mesh=mesh,
        in_specs=(
            P("seq", "head"),
            P("seq", "head"),
            P("seq", "head"),
            P("seq", "head"),
            P("head", None, None),
            P("head", None, None),
            P("head", None, None),
        ),
        out_specs=P("seq", "head"),
        check_vma=False,
    )
```

profile of v0, /device:TPU:22, one launch (start us, length us, event | category | flops | bytes accessed | tf_op | source)
XLA Modules:
  0.0 372.6 jit_solution(2090731207228613572)
XLA Ops:
  8.5 3.8 %collective-permute-start = (bf16[512,512]{1,0:T(8,128)(2,1)}, bf16[512,512]{1,0:T(8,128)(2,1)}, u32[]{:S(2)}, u32[]{:S(2)}) collective-permute-start(bf16[512,512]{1,0:T(8,128)(2,1)} %slice.33), channel_id=1, source_target_pairs={{0,1},{1,2},{2,3},{3,4},{4,5},{5,6},{6,7},{7,8},{8,9},{9,10},{10,1... | collective-permute-start | bytes 1572872 | tf_op jit(solution)/shard_map/ppermute | solution.py:18
  14.9 3.8 %collective-permute-start.1 = (bf16[512,512]{0,1:T(8,128)(2,1)}, bf16[512,512]{0,1:T(8,128)(2,1)}, u32[]{:S(2)}, u32[]{:S(2)}) collective-permute-start(bf16[512,512]{0,1:T(8,128)(2,1)} %slice.44), channel_id=1, source_target_pairs={{0,1},{1,2},{2,3},{3,4},{4,5},{5,6},{6,7},{7,8},{8,9},{9,10},{10,1... | collective-permute-start | bytes 1572872 | tf_op jit(solution)/shard_map/ppermute | solution.py:18
  19.2 2.4 convolution_bitcast_fusion.5
  24.4 2.3 fusion.82
  26.7 2.7 fusion.88
  29.4 2.3 fusion.73
  32.1 2.7 fusion.167
  45.9 2.8 pad_maximum_fusion.1
  55.5 2.9 pad_maximum_fusion
  58.4 8.1 %fusion.168 = (f32[4,512]{1,0:T(4,128)S(1)}, f32[4,512,1024]{1,2,0:T(8,128)}) fusion(pred[512,1024]{0,1:T(8,128)(4,1)} %and_and_fusion, bf16[512,4,128]{0,2,1:T(8,128)(2,1)} %bitcast.197, bf16[1024,4,128]{0,2,1:T(8,128)(2,1)} %bitcast.191), kind=kOutput, calls=%fused_computation.190 | convolution fusion | flops 545260544 | bytes 10493952 | tf_op jit(solution)/shard_map/sub | solution.py:128
  66.5 5.7 %fusion.17 = f32[4,512,128]{1,2,0:T(8,128)} fusion(bf16[1024,4,128]{0,2,1:T(8,128)(2,1)} %bitcast.194, f32[4,512,1024]{1,2,0:T(8,128)} %get-tuple-element.35, f32[4,512]{1,0:T(4,128)S(1)} %get-tuple-element.34), kind=kOutput, calls=%fused_computation.26 | convolution fusion | flops 541065216 | bytes 10493952 | tf_op jit(solution)/shard_map/hqk,khd->qhd/dot_general | solution.py:131
  72.2 6.4 %fusion.169 = (f32[4,512]{1,0:T(4,128)S(1)}, f32[4,512,1024]{1,2,0:T(8,128)}) fusion(pred[512,1024]{0,1:T(8,128)(4,1)} %and_and_fusion.1, bf16[512,4,128]{0,2,1:T(8,128)(2,1)S(1)} %bitcast.196, bf16[1024,4,128]{0,2,1:T(8,128)(2,1)S(1)} %bitcast.190), kind=kOutput, calls=%fused_computation.191 | convolution fusion | flops 545260544 | bytes 10493952 | tf_op jit(solution)/shard_map/sub | solution.py:128
  78.6 5.5 %fusion.16 = f32[4,512,128]{1,2,0:T(8,128)} fusion(bf16[1024,4,128]{0,2,1:T(8,128)(2,1)} %bitcast.193, f32[4,512,1024]{1,2,0:T(8,128)} %get-tuple-element.37, f32[4,512]{1,0:T(4,128)S(1)} %get-tuple-element.36), kind=kOutput, calls=%fused_computation.25 | convolution fusion | flops 541065216 | bytes 10493952 | tf_op jit(solution)/shard_map/hqk,khd->qhd/dot_general | solution.py:131
  84.1 100.0 %all-reduce.7.cloned.1.call-done = (bf16[1,512,512]{2,1,0:T(8,128)(2,1)}, bf16[1,512,512]{2,1,0:T(8,128)(2,1)}, bf16[1,512,512]{2,1,0:T(8,128)(2,1)}) async-done(((bf16[1,512,512]{2,1,0:T(8,128)(2,1)}, bf16[1,512,512]{2,1,0:T(8,128)(2,1)}, bf16[1,512,512]{2,1,0:T(8,128)(2,1)}), (bf16[1,512,512]{2,1,0:T(8,128)(2,1)}, bf16[1,512,512]{2,1,0:T(8,128)(2,1)}, ...) | async-done | bytes 1572880 | tf_op jit(solution)/shard_map/psum | solution.py:68
  192.1 2.4 fusion.76
  194.5 2.7 fusion.85
  197.2 2.3 fusion.79
  199.5 8.4 %fusion.170 = (f32[4,512]{1,0:T(4,128)S(1)}, f32[4,512,1024]{1,2,0:T(8,128)}) fusion(pred[512,1024]{0,1:T(8,128)(4,1)} %and_and_fusion.2, bf16[1024,4,128]{0,2,1:T(8,128)(2,1)} %bitcast.189, bf16[512,4,128]{0,2,1:T(8,128)(2,1)} %bitcast.195), kind=kOutput, calls=%fused_computation.192 | convolution fusion | flops 545260544 | bytes 10493952 | tf_op jit(solution)/shard_map/sub | solution.py:128
  208.0 5.3 %fusion.15 = f32[4,128,512]{2,1,0:T(8,128)} fusion(bf16[1024,4,128]{0,2,1:T(8,128)(2,1)S(1)} %bitcast.192, f32[4,512,1024]{1,2,0:T(8,128)} %get-tuple-element.39, f32[4,512]{1,0:T(4,128)S(1)} %get-tuple-element.38), kind=kOutput, calls=%fused_computation.24 | convolution fusion | flops 541065216 | bytes 10493952 | tf_op jit(solution)/shard_map/hqk,khd->qhd/dot_general | solution.py:131
  213.3 136.3 %all-reduce.5.cloned.1.call-done = (bf16[1,512,512]{2,1,0:T(8,128)(2,1)}, bf16[1,512,512]{2,1,0:T(8,128)(2,1)}, bf16[1,512,512]{2,1,0:T(8,128)(2,1)}) async-done(((bf16[1,512,512]{2,1,0:T(8,128)(2,1)}, bf16[1,512,512]{2,1,0:T(8,128)(2,1)}, bf16[1,512,512]{2,1,0:T(8,128)(2,1)}), (bf16[1,512,512]{2,1,0:T(8,128)(2,1)}, bf16[1,512,512]{2,1,0:T(8,128)(2,1)}, ...) | async-done | bytes 1572880 | tf_op jit(solution)/shard_map/psum | solution.py:68
  349.6 3.0 multiply_reduce_fusion.1
  353.1 2.8 convolution_bitcast_fusion.1
  355.9 7.3 %fusion.27 = bf16[1536,512]{0,1:T(8,128)(2,1)} fusion(f32[512,512]{0,1:T(8,128)} %bitcast.198, f32[512,512]{0,1:T(8,128)} %bitcast.199, f32[512,512]{0,1:T(8,128)} %bitcast.200, f32[1536,1,512]{2,0,1:T(8,128)} %convolution_bitcast_fusion.1, bf16[1,512,512]{2,1,0:T(8,128)(2,1)} %get-tuple-element.20, f32[512]{0:T(512)S(1)} %add_sqrt_fusion.2, ...), kind=kOutput, calls=%fused_computation.51 | convolution fusion | flops 1628176384 | bytes 13654017 | tf_op jit(solution)/shard_map/nhf,hfe->nhe/dot_general | solution.py:61
  363.2 2.6 copy.48
  (97 shorter events, 34.2 us)
Async XLA Ops:
  6.5 12.2 %copy-start.3 = (bf16[1536,512]{1,0:T(8,128)(2,1)S(1)}, bf16[1536,512]{1,0:T(8,128)(2,1)}, u32[]{:S(2)}) copy-start(bf16[1536,512]{1,0:T(8,128)(2,1)} %param.8) | copy-start | bytes 4718596
  6.5 177.6 %all-reduce.7.cloned.1.call-start = ((), (), s32[]{:S(2)}) async-start(), calls=%async_computation.1 | async-start | bytes 3145728 | tf_op jit(solution)/shard_map/psum | solution.py:68
  8.5 37.3 %collective-permute-start = (bf16[512,512]{1,0:T(8,128)(2,1)}, bf16[512,512]{1,0:T(8,128)(2,1)}, u32[]{:S(2)}, u32[]{:S(2)}) collective-permute-start(bf16[512,512]{1,0:T(8,128)(2,1)} %slice.33), channel_id=1, source_target_pairs={{0,1},{1,2},{2,3},{3,4},{4,5},{5,6},{6,7},{7,8},{8,9},{9,10},{10,1... | collective-permute-start | bytes 1572872 | tf_op jit(solution)/shard_map/ppermute | solution.py:18
  14.9 40.6 %collective-permute-start.1 = (bf16[512,512]{0,1:T(8,128)(2,1)}, bf16[512,512]{0,1:T(8,128)(2,1)}, u32[]{:S(2)}, u32[]{:S(2)}) collective-permute-start(bf16[512,512]{0,1:T(8,128)(2,1)} %slice.44), channel_id=1, source_target_pairs={{0,1},{1,2},{2,3},{3,4},{4,5},{5,6},{6,7},{7,8},{8,9},{9,10},{10,1... | collective-permute-start | bytes 1572872 | tf_op jit(solution)/shard_map/ppermute | solution.py:18
  19.2 2.4 copy-start.4
  19.2 2.4 copy-start.10
  21.7 1.4 copy-start
  21.7 1.7 copy-start.1
  31.7 317.8 %all-reduce.5.cloned.1.call-start = ((), (), s32[]{:S(2)}) async-start(), calls=%async_computation | async-start | bytes 3145728 | tf_op jit(solution)/shard_map/psum | solution.py:68
  32.0 2.7 copy-start.6
  66.5 5.7 %copy-start.16 = (bf16[1024,512]{0,1:T(8,128)(2,1)S(1)}, bf16[1024,512]{0,1:T(8,128)(2,1)}, u32[]{:S(2)}) copy-start(bf16[1024,512]{0,1:T(8,128)(2,1)} %get-tuple-element.30) | copy-start | bytes 3145732
  66.5 5.7 %copy-start.18 = (bf16[512,512]{0,1:T(8,128)(2,1)S(1)}, bf16[512,512]{0,1:T(8,128)(2,1)}, u32[]{:S(2)}) copy-start(bf16[512,512]{0,1:T(8,128)(2,1)} %copy.66) | copy-start | bytes 1572868
  78.6 107.3 %copy-start.2 = (f32[1,512,512]{2,1,0:T(8,128)S(1)}, f32[1,512,512]{2,1,0:T(8,128)}, u32[]{:S(2)}) copy-start(f32[1,512,512]{2,1,0:T(8,128)} %param.12) | copy-start | bytes 3145732
  184.2 3.1 copy-start.13
  184.2 4.6 %copy-start.5 = (bf16[1536,512]{1,0:T(8,128)(2,1)S(1)}, bf16[1536,512]{1,0:T(8,128)(2,1)}, u32[]{:S(2)}) copy-start(bf16[1536,512]{1,0:T(8,128)(2,1)} %param.8) | copy-start | bytes 4718596
  184.2 4.6 %copy-start.8 = (f32[1,512,512]{2,1,0:T(8,128)S(1)}, f32[1,512,512]{2,1,0:T(8,128)}, u32[]{:S(2)}) copy-start(f32[1,512,512]{2,1,0:T(8,128)} %param.11) | copy-start | bytes 3145732
  184.2 4.6 %copy-start.14 = (bf16[1,512,512]{2,1,0:T(8,128)(2,1)S(1)}, bf16[1,512,512]{2,1,0:T(8,128)(2,1)}, u32[]{:S(2)}) copy-start(bf16[1,512,512]{2,1,0:T(8,128)(2,1)} %get-tuple-element.22) | copy-start | bytes 1572868
  188.8 1.2 copy-start.11
  199.5 8.5 %copy-start.17 = (bf16[1024,512]{0,1:T(8,128)(2,1)S(1)}, bf16[1024,512]{0,1:T(8,128)(2,1)}, u32[]{:S(2)}) copy-start(bf16[1024,512]{0,1:T(8,128)(2,1)} %copy.27) | copy-start | bytes 3145732
  349.6 3.1 copy-start.19
  349.6 3.5 copy-start.7
  349.6 3.5 copy-start.9
  349.6 3.5 copy-start.15
  349.6 3.5 copy-start.20
  (2 other events, 2.1 us)
Sparse Core Ops, SparseCore 0:
  31.9 152.2 all-reduce.6
  199.7 149.8 all-reduce.4
where the time goes:
time: 375 us; the launch traced here: 373 us
  waiting for transfers between devices  236 us (63%)
  matrix products  71.9 us (19%)
  local copies, waits for them, and re-layouts  23.6 us (6%)
  other arithmetic  19.1 us (5%)
  between operations  13.8 us (4%)
  starting transfers between devices  7.85 us (2%)
    psum x2, waiting for transfers between devices, renew(): lax.psum(grad_terms[0].astype(jnp.bfloat16), 'seq').astype(jnp.float32)  236 us
    sub x3, matrix products, on_device(): expo = jnp.exp(scores - top_score)  22.9 us
    dot_general x3, matrix products, on_device(): jnp.einsum('hqk,khd->qhd', attend, value_block, preferred_element_type=jn...  16.5 us
    unnamed x48, local copies, waits for them, and re-layouts  8.7 us
    reduce_sum x5, other arithmetic, rescale(): target_norm = jnp.sqrt(jnp.sum(weight * weight, axis=-2, keepdims=True))  7.86 us
    ppermute x2, starting transfers between devices, shifted(): return lax.ppermute(block, axis, route)  7.63 us
  transfers between devices with their start and end apart: 4, of which 2 were waited for; matrix products, arithmetic and copies ran while one was open for 22% of the time, Pallas kernels for 0%

commit v1 on v0

v1 whole, which is shorter than its diff:
```python
import functools
import math

import jax
import jax.numpy as jnp
from jax import lax
from jax.experimental import pallas as pl
from jax.experimental.pallas import tpu as pltpu
from jax.sharding import PartitionSpec as P

AH = 128
WINDOW = 512
TILE = 256
NZ = 8
NY = 4
EPSILON = 1e-06
MESH = pl.DeviceIdType.MESH
HOPS = ((4, 3), (3, 4), (4, 3))
F32 = jnp.float32
BF16 = jnp.bfloat16


def dot_nn(a, b):
    return lax.dot_general(a, b, (((1,), (0,)), ((), ())), preferred_element_type=F32)


def dot_nt(a, b):
    return lax.dot_general(a, b, (((1,), (1,)), ((), ())), preferred_element_type=F32)


def norm_rows(rows):
    as_float = rows.astype(F32)
    mean = jnp.mean(as_float * as_float, axis=-1, keepdims=True)
    return (as_float / jnp.sqrt(mean + EPSILON)).astype(BF16)


def kernel(
    q_hbm, k_hbm, v_hbm, rate_hbm, gate_hbm, down_hbm, up_hbm, out_hbm,
    q_ref, k_ref, v_ref, rate_ref, w0_ref, w0t_ref, kn_ref, wa_ref, wdn_ref, wb_ref, wc_ref,
    hid_ref, g_ref, rs_send, rs_recv, ysend, yrecv, up_recv, up_pair, att_ref, out_ref,
    load_sem, out_sem, halo_ssem, halo_rsem, rs_ssem, rs_rsem, y_ssem, y_rsem, up_ssem, up_rsem,
    pair_ssem, pair_rsem, aga_ssem, aga_rsem, agb_ssem, agb_rsem,
):
    rows, width = q_hbm.shape
    chunk = width // NZ
    head = lax.axis_index("head")
    seq = lax.axis_index("seq")
    y = seq // NZ
    z = seq % NZ
    upper = y >= NY // 2
    lower = y < NY // 2
    last = NZ * NY - 1
    z_next = y * NZ + lax.rem(z + 1, NZ)
    z_prev = y * NZ + lax.rem(z + NZ - 1, NZ)
    pair = (y + 1 - 2 * lax.rem(y, 2)) * NZ + z
    across = (NY - 1 - y) * NZ + z
    heads = width // AH
    tiles = rows // TILE

    def signal(target):
        pl.semaphore_signal(pltpu.get_barrier_semaphore(), inc=1, device_id=(head, target), device_id_type=MESH)

    def remote(src, dst, ssem, rsem, target):
        return pltpu.make_async_remote_copy(
            src_ref=src, dst_ref=dst, send_sem=ssem, recv_sem=rsem, device_id=(head, target), device_id_type=MESH
        )

    loads = [
        pltpu.make_async_copy(k_hbm, k_ref.at[pl.ds(WINDOW, rows)], load_sem.at[0]),
        pltpu.make_async_copy(gate_hbm.at[0], w0_ref.at[1], load_sem.at[1]),
        pltpu.make_async_copy(up_hbm.at[0], w0_ref.at[2], load_sem.at[2]),
        pltpu.make_async_copy(down_hbm.at[0], w0_ref.at[0], load_sem.at[3]),
        pltpu.make_async_copy(v_hbm, v_ref.at[pl.ds(WINDOW, rows)], load_sem.at[4]),
        pltpu.make_async_copy(rate_hbm, rate_ref, load_sem.at[5]),
        pltpu.make_async_copy(q_hbm, q_ref, load_sem.at[6]),
    ]
    for load in loads:
        load.start()

    for target in (z_next, z_prev, pair, across):
        signal(target)
    edge_next = jnp.logical_and(z == NZ - 1, y < NY - 1)
    edge_prev = jnp.logical_and(z == 0, y > 0)

    @pl.when(edge_next)
    def _():
        signal(seq + 1)

    @pl.when(edge_prev)
    def _():
        signal(seq - 1)

    for index, load in ((1, loads[1]), (2, loads[2]), (0, loads[3])):
        load.wait()
        w0t_ref[index] = w0_ref[index].T
    loads[0].wait()

    def norm_keys(tile, carry):
        at = pl.multiple_of(tile * TILE, TILE)
        kn_ref[pl.ds(at, TILE), :] = norm_rows(k_ref[pl.ds(at + WINDOW, TILE), :])
        return carry

    lax.fori_loop(0, tiles, norm_keys, 0)
    for load in loads[4:]:
        load.wait()

    pl.semaphore_wait(
        pltpu.get_barrier_semaphore(), 4 + edge_next.astype(jnp.int32) + edge_prev.astype(jnp.int32)
    )

    halo = [
        remote(
            ref.at[pl.ds(rows, WINDOW)], ref.at[pl.ds(0, WINDOW)], halo_ssem.at[i], halo_rsem.at[i],
            lax.rem(seq + 1, NZ * NY),
        )
        for i, ref in enumerate((k_ref, v_ref))
    ]

    @pl.when(seq == 0)
    def _():
        k_ref[pl.ds(0, WINDOW), :] = jnp.zeros((WINDOW, width), BF16)
        v_ref[pl.ds(0, WINDOW), :] = jnp.zeros((WINDOW, width), BF16)

    def attention_tile(tile, carry):
        at = pl.multiple_of(tile * TILE, TILE)
        row = lax.broadcasted_iota(jnp.int32, (TILE, TILE), 0)
        col = lax.broadcasted_iota(jnp.int32, (TILE, TILE), 1)
        recent = col <= row
        real0 = jnp.logical_or(seq > 0, at >= WINDOW)
        real1 = jnp.logical_or(seq > 0, at + TILE >= WINDOW)
        scale = math.log2(math.e) / math.sqrt(AH)
        for a in range(heads):
            lanes = slice(a * AH, (a + 1) * AH)
            q = q_ref[pl.ds(at, TILE), lanes]
            s0 = dot_nt(q, k_ref[pl.ds(at, TILE), lanes])
            s1 = dot_nt(q, k_ref[pl.ds(at + TILE, TILE), lanes])
            s2 = dot_nt(q, k_ref[pl.ds(at + 2 * TILE, TILE), lanes])
            edge = jnp.where(recent, s2, jnp.where(real0, s0, -1e30))
            middle = jnp.where(real1, s1, -1e30)
            top = jnp.max(jnp.maximum(edge, middle), axis=-1, keepdims=True)
            edge = jnp.exp2((edge - top) * scale)
            middle = jnp.exp2((middle - top) * scale)
            total = jnp.sum(edge + middle, axis=-1, keepdims=True)
            out = dot_nn(middle.astype(BF16), v_ref[pl.ds(at + TILE, TILE), lanes])
            out += dot_nn(jnp.where(recent, edge, 0.0).astype(BF16), v_ref[pl.ds(at + 2 * TILE, TILE), lanes])
            out += dot_nn(jnp.where(recent, 0.0, edge).astype(BF16), v_ref[pl.ds(at, TILE), lanes])
            att_ref[pl.ds(at, TILE), lanes] = out / total
        return carry

    def attention():
        inner = WINDOW // TILE
        lax.fori_loop(inner, tiles, attention_tile, 0)

        @pl.when(seq > 0)
        def _():
            for copy in halo:
                copy.wait_recv()

        lax.fori_loop(0, inner, attention_tile, 0)

    def update(index, old, step):
        moved = old + step
        before = jnp.sum(old * old, axis=-1, keepdims=True)
        after = jnp.sum(moved * moved, axis=-1, keepdims=True)
        return moved * (jnp.sqrt(before) / jnp.sqrt(after + EPSILON))

    def rows_of(position):
        return pl.ds(pl.multiple_of(lax.rem(position + 2 * NZ, NZ) * chunk, chunk), chunk)

    own = rows_of(z)
    signs = (1, -1)
    ring = (z_next, z_prev)

    def gather_send(ref, ssem, rsem, index, way, step):
        part = ref.at[index, rows_of(z - signs[way] * step)]
        return remote(part, part, ssem.at[index, way, step], rsem.at[index, way, step], ring[way])

    def gather_take(ref, ssem, rsem, index, way, step):
        part = ref.at[index, rows_of(z - signs[way] * (step + 1))]
        return remote(part, part, ssem.at[index, way, step], rsem.at[index, way, step], ring[way])

    def gather_rest(ref, ssem, rsem):
        for step in range(1, 5):
            for index in range(3):
                for way in range(2):
                    if step <= HOPS[index][way]:
                        gather_take(ref, ssem, rsem, index, way, step - 1).wait_recv()
                        if step < HOPS[index][way]:
                            gather_send(ref, ssem, rsem, index, way, step).start()

    def gather_drain(ref, ssem, rsem):
        for index in range(3):
            for way in range(2):
                for step in range(HOPS[index][way]):
                    gather_send(ref, ssem, rsem, index, way, step).wait_send()

    up_copies = [remote(ysend.at[i], up_recv.at[i], up_ssem.at[i], up_rsem.at[i], across) for i in range(3)]
    pair_copies = [remote(up_recv.at[i], up_pair.at[i], pair_ssem.at[i], pair_rsem.at[i], pair) for i in range(3)]
    y_copies = [remote(ysend.at[i], yrecv.at[i], y_ssem.at[i], y_rsem.at[i], pair) for i in range(3)]

    @pl.when(jnp.logical_and(seq >= NZ * NY // 2 - 1, seq < last))
    def _():
        for copy in halo:
            copy.start()

    @pl.when(lower)
    def _():
        wa_ref[1] = w0t_ref[1].astype(BF16)
        wa_ref[2] = w0t_ref[2].astype(BF16)
        wdn_ref[...] = w0_ref[0].astype(BF16)
        for index in range(3):
            wc_ref[index] = w0t_ref[index, own, :]

    @pl.when(upper)
    def _():
        attention()
        for index in range(3):
            up_copies[index].wait_recv()
            pair_copies[index].start()
        for index in range(3):
            pair_copies[index].wait_recv()
            step = up_recv[index].astype(F32) + up_pair[index].astype(F32)
            fresh = update(index, w0t_ref[index, own, :], step)
            wc_ref[index] = fresh
            wa_ref[index, own, :] = fresh.astype(BF16)
            for way in range(2):
                gather_send(wa_ref, aga_ssem, aga_rsem, index, way, 0).start()
        gather_rest(wa_ref, aga_ssem, aga_rsem)
        gather_drain(wa_ref, aga_ssem, aga_rsem)
        for index in range(3):
            pair_copies[index].wait_send()
        wdn_ref[...] = wa_ref[0].T

    def grad_tile(tile, carry):
        at = pl.multiple_of(tile * TILE, TILE)
        keys = kn_ref[pl.ds(at, TILE), :]
        gate_pre = dot_nt(wa_ref[1], keys)
        up_pre = dot_nt(wa_ref[2], keys)
        rate = rate_ref[0:1, pl.ds(at, TILE)].astype(F32)
        grad = dot_nt(wdn_ref[...], v_ref[pl.ds(at + WINDOW, TILE), :]) * rate
        sig = jax.nn.sigmoid(gate_pre)
        act = gate_pre * sig
        hid_ref[0, :, pl.ds(at, TILE)] = (act * up_pre * rate).astype(BF16)
        hid_ref[1, :, pl.ds(at, TILE)] = (grad * up_pre * sig * (1.0 + gate_pre * (1.0 - sig))).astype(BF16)
        hid_ref[2, :, pl.ds(at, TILE)] = (grad * act).astype(BF16)
        return carry

    lax.fori_loop(0, tiles, grad_tile, 0)

    def rs_copy(index, way, step):
        return remote(
            rs_send.at[index, way, step], rs_recv.at[index, way, step],
            rs_ssem.at[index, way, step], rs_rsem.at[index, way, step], ring[way],
        )

    def scatter_step(index, way, step):
        hops = HOPS[index][way]
        if step >= hops:
            return
        value = g_ref[index, rows_of(z + signs[way] * (hops - step)), :]
        if step > 0:
            rs_copy(index, way, step - 1).wait_recv()
            value = value + rs_recv[index, way, step - 1].astype(F32)
        rs_send[index, way, step] = value.astype(BF16)
        rs_copy(index, way, step).start()

    g_ref[0] = dot_nn(hid_ref[0], v_ref[pl.ds(WINDOW, rows), :]).T
    scatter_step(0, 0, 0)
    scatter_step(0, 1, 0)
    g_ref[1] = dot_nn(hid_ref[1], kn_ref[...])
    scatter_step(1, 0, 0)
    scatter_step(1, 1, 0)
    g_ref[2] = dot_nn(hid_ref[2], kn_ref[...])
    scatter_step(2, 0, 0)
    scatter_step(2, 1, 0)
    for step in range(1, 4):
        for index in range(3):
            for way in range(2):
                scatter_step(index, way, step)
    for index in range(3):
        value = g_ref[index, own, :]
        for way in range(2):
            final = HOPS[index][way] - 1
            rs_copy(index, way, final).wait_recv()
            value = value + rs_recv[index, way, final].astype(F32)
        ysend[index] = value.astype(BF16)
        y_copies[index].start()

        @pl.when(lower)
        def _():
            up_copies[index].start()

    @pl.when(seq < NZ * NY // 2 - 1)
    def _():
        for copy in halo:
            copy.start()

    for index in range(3):
        y_copies[index].wait_recv()
        step = ysend[index].astype(F32) + yrecv[index].astype(F32)
        wb_ref[index, own, :] = update(index, wc_ref[index], step).astype(BF16)
        for way in range(2):
            gather_send(wb_ref, agb_ssem, agb_rsem, index, way, 0).start()
    gather_rest(wb_ref, agb_ssem, agb_rsem)

    @pl.when(lower)
    def _():
        attention()

    out_copies = []

    def apply_tile(tile, carry):
        at = pl.multiple_of(tile * TILE, TILE)
        queries = norm_rows(q_ref[pl.ds(at, TILE), :])
        gate_pre = dot_nt(queries, wb_ref[1])
        up_pre = dot_nt(queries, wb_ref[2])
        hidden = (gate_pre * jax.nn.sigmoid(gate_pre) * up_pre).astype(BF16)
        fast = dot_nt(hidden, wb_ref[0]).astype(BF16)
        out_ref[pl.ds(at, TILE), :] = (fast.astype(F32) + att_ref[pl.ds(at, TILE), :]).astype(BF16)
        pltpu.make_async_copy(
            out_ref.at[pl.ds(at, TILE)], out_hbm.at[pl.ds(at, TILE)], out_sem.at[tile]
        ).start()
        return carry

    lax.fori_loop(0, tiles, apply_tile, 0)

    gather_drain(wb_ref, agb_ssem, agb_rsem)
    for index in range(3):
        for way in range(2):
            for step in range(HOPS[index][way]):
                rs_copy(index, way, step).wait_send()
        y_copies[index].wait_send()

    @pl.when(lower)
    def _():
        for index in range(3):
            up_copies[index].wait_send()

    @pl.when(seq < last)
    def _():
        for copy in halo:
            copy.wait_send()

    for tile in range(tiles):
        at = tile * TILE
        pltpu.make_async_copy(
            out_ref.at[pl.ds(at, TILE)], out_hbm.at[pl.ds(at, TILE)], out_sem.at[tile]
        ).wait()


def on_device(queries, key_rows, value_rows, learn_rates, gate_fast, down_fast, up_fast):
    rows, width = queries.shape
    chunk = width // NZ
    tiles = rows // TILE
    dma = pltpu.SemaphoreType.DMA
    square = (3, width, width)
    parts = (3, 2, 4, chunk, width)
    return pl.pallas_call(
        kernel,
        name="layer",
        out_shape=jax.ShapeDtypeStruct((rows, width), BF16),
        in_specs=[pl.BlockSpec(memory_space=pl.ANY)] * 7,
        out_specs=pl.BlockSpec(memory_space=pl.ANY),
        scratch_shapes=[
            pltpu.VMEM((rows, width), BF16),
            pltpu.VMEM((WINDOW + rows, width), BF16),
            pltpu.VMEM((WINDOW + rows, width), BF16),
            pltpu.VMEM((1, rows), BF16),
            pltpu.VMEM(square, F32),
            pltpu.VMEM(square, F32),
            pltpu.VMEM((rows, width), BF16),
            pltpu.VMEM(square, BF16),
            pltpu.VMEM(square[1:], BF16),
            pltpu.VMEM(square, BF16),
            pltpu.VMEM((3, chunk, width), F32),
            pltpu.VMEM((3, width, rows), BF16),
            pltpu.VMEM(square, F32),
            pltpu.VMEM(parts, BF16),
            pltpu.VMEM(parts, BF16),
            pltpu.VMEM((3, chunk, width), BF16),
            pltpu.VMEM((3, chunk, width), BF16),
            pltpu.VMEM((3, chunk, width), BF16),
            pltpu.VMEM((3, chunk, width), BF16),
            pltpu.VMEM((rows, width), F32),
            pltpu.VMEM((rows, width), BF16),
            dma((7,)),
            dma((tiles,)),
            dma((2,)),
            dma((2,)),
            dma((3, 2, 4)),
            dma((3, 2, 4)),
            dma((3,)),
            dma((3,)),
            dma((3,)),
            dma((3,)),
            dma((3,)),
            dma((3,)),
            dma((3, 2, 4)),
            dma((3, 2, 4)),
            dma((3, 2, 4)),
            dma((3, 2, 4)),
        ],
        compiler_params=pltpu.CompilerParams(
            collective_id=0, has_side_effects=True, vmem_limit_bytes=60 * 1024 * 1024
        ),
    )(queries, key_rows, value_rows, learn_rates.T, gate_fast, down_fast, up_fast)


def solution(mesh):
    return jax.shard_map(
        on_device,
        mesh=mesh,
        in_specs=(
            P("seq", "head"),
            P("seq", "head"),
            P("seq", "head"),
            P("seq", "head"),
            P("head", None, None),
            P("head", None, None),
            P("head", None, None),
        ),
        out_specs=P("seq", "head"),
        check_vma=False,
    )
```

time: 375 us -> 121 us (0.32)
  waiting for transfers between devices: 236 us -> 0 us
  Pallas kernels: 0 us -> 119 us
  matrix products: 71.9 us -> 0 us
  local copies, waits for them, and re-layouts: 23.6 us -> 2.65 us
  other arithmetic: 19.1 us -> 0 us
  between operations: 13.8 us -> 0.01 us
  starting transfers between devices: 7.85 us -> 0 us
    psum x2 -> x0, waiting for transfers between devices: 236 us -> none  [renew(): lax.psum(grad_terms[0].astype(jnp.bfloat16), 'seq').astype(jnp.float32)]
    pallas_call x0 -> x1, Pallas kernels: none -> 119 us  [on_device(): pl.pallas_call(kernel, name='layer', out_shape=jax.ShapeDtypeStruct((rows...]
    dot_general x17 -> x0, matrix products: 48.9 us -> none  [the longest x3 16.5 us: on_device(): jnp.einsum('hqk,khd->qhd', attend, value_block, preferred_element_type=jn...]
    sub x3 -> x0, matrix products: 22.9 us -> none  [on_device(): expo = jnp.exp(scores - top_score)]
    slice x6 -> x0, local copies, waits for them, and re-layouts: 12.3 us -> none  [the longest x3 6.83 us: on_device(): wide_values[lower:lower + 2 * WINDOW].reshape(2 * WINDOW, attn_heads, AH)]
    reduce_sum x7 -> x0, other arithmetic: 8.61 us -> none  [the longest x5 7.86 us: rescale(): target_norm = jnp.sqrt(jnp.sum(weight * weight, axis=-2, keepdims=True))]
    ppermute x2 -> x0, starting transfers between devices: 7.63 us -> none  [shifted(): return lax.ppermute(block, axis, route)]
    unnamed x48 -> x1, local copies, waits for them, and re-layouts: 8.7 us -> 2.65 us
  transfers between devices with their start and end apart: 4 -> 0, of which waited for: 2 -> 0; matrix products, arithmetic and copies ran while one was open for 22% -> 0% of each run, Pallas kernels for 0% -> 0%
where the time goes in v1:
time: 121 us
  Pallas kernels  119 us (98%)
  local copies, waits for them, and re-layouts  2.65 us (2%)
    pallas_call x1, Pallas kernels, on_device(): pl.pallas_call(kernel, name='layer', out_shape=jax.ShapeDtypeStruct((rows...  119 us
    unnamed x1, local copies, waits for them, and re-layouts  2.65 us

profile of v1, /device:TPU:22, one launch (start us, length us, event | category | flops | bytes accessed | tf_op | source)
XLA Modules:
  0.0 121.2 jit_solution(2847620084775291992)
XLA Ops:
  0.0 118.6 %layer.1 = bf16[1536,512]{1,0:T(8,128)(2,1)} custom-call(bf16[1536,512]{1,0:T(8,128)(2,1)} %q_hbm.1, bf16[1536,512]{1,0:T(8,128)(2,1)} %k_hbm.1, bf16[1536,512]{1,0:T(8,128)(2,1)} %v_hbm.1, bf16[1,1536]{1,0:T(2,128)(2,1)} %bitcast.1, f32[1,512,512]{2,1,0:T(8,128)} %gate_hbm.1, f32[1,512,512]{2,1,0:T(8,128)} %down_hbm.1, f32[1,512,512]{2,1,0:T(8,128)} %up_hbm.1), custom_call_target="tpu_custom_call" | custom-call | tf_op jit(solution)/shard_map/layer/pallas_call | solution.py:358
  118.6 2.7 %copy.9 = bf16[1536,512]{1,0:T(8,128)(2,1)} copy(bf16[1536,512]{1,0:T(8,128)(2,1)} %layer.1) | data formatting | bytes 3145728

commit v2 on v1

v2 whole, which is shorter than its diff:
```python
import functools
import math

import jax
import jax.numpy as jnp
from jax import lax
from jax.experimental import pallas as pl
from jax.experimental.pallas import tpu as pltpu
from jax.sharding import PartitionSpec as P

AH = 128
WINDOW = 512
TILE = 256
NZ = 8
NY = 4
EPSILON = 1e-06
MESH = pl.DeviceIdType.MESH
SPLIT = 2
PIECES = tuple((index, part) for index in range(3) for part in range(SPLIT))


def hops_of(part, way):
    return 4 - (part + way) % 2


F32 = jnp.float32
BF16 = jnp.bfloat16


def dot_nn(a, b):
    return lax.dot_general(a, b, (((1,), (0,)), ((), ())), preferred_element_type=F32)


def dot_nt(a, b):
    return lax.dot_general(a, b, (((1,), (1,)), ((), ())), preferred_element_type=F32)


def norm_rows(rows):
    as_float = rows.astype(F32)
    mean = jnp.mean(as_float * as_float, axis=-1, keepdims=True)
    return (as_float / jnp.sqrt(mean + EPSILON)).astype(BF16)


def kernel(
    q_hbm, k_hbm, v_hbm, rate_hbm, gate_hbm, down_hbm, up_hbm, out_hbm,
    q_ref, k_ref, v_ref, rate_ref, w0_ref, w0t_ref, kn_ref, wa_ref, wdn_ref, wb_ref, wc_ref,
    hid_ref, g_ref, rs_send, rs_recv, ysend, yrecv, up_recv, up_pair, att_ref, out_ref,
    load_sem, out_sem, halo_ssem, halo_rsem, rs_ssem, rs_rsem, y_ssem, y_rsem, up_ssem, up_rsem,
    pair_ssem, pair_rsem, aga_ssem, aga_rsem, agb_ssem, agb_rsem,
):
    rows, width = q_hbm.shape
    chunk = width // NZ
    piece = chunk // SPLIT
    head = lax.axis_index("head")
    seq = lax.axis_index("seq")
    y = seq // NZ
    z = seq % NZ
    upper = y >= NY // 2
    lower = y < NY // 2
    last = NZ * NY - 1
    z_next = y * NZ + lax.rem(z + 1, NZ)
    z_prev = y * NZ + lax.rem(z + NZ - 1, NZ)
    pair = (y + 1 - 2 * lax.rem(y, 2)) * NZ + z
    across = (NY - 1 - y) * NZ + z
    heads = width // AH
    tiles = rows // TILE

    def signal(target):
        pl.semaphore_signal(pltpu.get_barrier_semaphore(), inc=1, device_id=(head, target), device_id_type=MESH)

    def remote(src, dst, ssem, rsem, target):
        return pltpu.make_async_remote_copy(
            src_ref=src, dst_ref=dst, send_sem=ssem, recv_sem=rsem, device_id=(head, target), device_id_type=MESH
        )

    loads = [
        pltpu.make_async_copy(k_hbm, k_ref.at[pl.ds(WINDOW, rows)], load_sem.at[0]),
        pltpu.make_async_copy(gate_hbm.at[0], w0_ref.at[1], load_sem.at[1]),
        pltpu.make_async_copy(up_hbm.at[0], w0_ref.at[2], load_sem.at[2]),
        pltpu.make_async_copy(down_hbm.at[0], w0_ref.at[0], load_sem.at[3]),
        pltpu.make_async_copy(v_hbm, v_ref.at[pl.ds(WINDOW, rows)], load_sem.at[4]),
        pltpu.make_async_copy(rate_hbm, rate_ref, load_sem.at[5]),
        pltpu.make_async_copy(q_hbm, q_ref, load_sem.at[6]),
    ]
    for load in (loads[0], loads[1], loads[2], loads[4], loads[5], loads[3]):
        load.start()

    for target in (z_next, z_prev, pair, across):
        signal(target)
    edge_next = jnp.logical_and(z == NZ - 1, y < NY - 1)
    edge_prev = jnp.logical_and(z == 0, y > 0)

    @pl.when(edge_next)
    def _():
        signal(seq + 1)

    @pl.when(edge_prev)
    def _():
        signal(seq - 1)

    def norm_keys(tile, carry):
        at = pl.multiple_of(tile * TILE, TILE)
        kn_ref[pl.ds(at, TILE), :] = norm_rows(k_ref[pl.ds(at + WINDOW, TILE), :])
        return carry

    loads[0].wait()
    lax.fori_loop(0, tiles, norm_keys, 0)
    for index, load in ((1, loads[1]), (2, loads[2]), (0, loads[3])):
        load.wait()
        w0t_ref[index] = w0_ref[index].T
    loads[6].start()
    loads[4].wait()
    loads[5].wait()

    pl.semaphore_wait(
        pltpu.get_barrier_semaphore(), 4 + edge_next.astype(jnp.int32) + edge_prev.astype(jnp.int32)
    )

    halo = [
        remote(
            ref.at[pl.ds(rows, WINDOW)], ref.at[pl.ds(0, WINDOW)], halo_ssem.at[i], halo_rsem.at[i],
            lax.rem(seq + 1, NZ * NY),
        )
        for i, ref in enumerate((k_ref, v_ref))
    ]

    @pl.when(seq == 0)
    def _():
        k_ref[pl.ds(0, WINDOW), :] = jnp.zeros((WINDOW, width), BF16)
        v_ref[pl.ds(0, WINDOW), :] = jnp.zeros((WINDOW, width), BF16)

    def attend(tile, a):
        at = pl.multiple_of(tile * TILE, TILE)
        row = lax.broadcasted_iota(jnp.int32, (TILE, TILE), 0)
        col = lax.broadcasted_iota(jnp.int32, (TILE, TILE), 1)
        recent = col <= row
        real0 = jnp.logical_or(seq > 0, at >= WINDOW)
        real1 = jnp.logical_or(seq > 0, at + TILE >= WINDOW)
        scale = math.log2(math.e) / math.sqrt(AH)
        lanes = slice(a * AH, (a + 1) * AH)
        q = q_ref[pl.ds(at, TILE), lanes]
        s0 = dot_nt(q, k_ref[pl.ds(at, TILE), lanes])
        s1 = dot_nt(q, k_ref[pl.ds(at + TILE, TILE), lanes])
        s2 = dot_nt(q, k_ref[pl.ds(at + 2 * TILE, TILE), lanes])
        edge = jnp.where(recent, s2, jnp.where(real0, s0, -1e30))
        middle = jnp.where(real1, s1, -1e30)
        top = jnp.max(jnp.maximum(edge, middle), axis=-1, keepdims=True)
        edge = jnp.exp2((edge - top) * scale)
        middle = jnp.exp2((middle - top) * scale)
        total = jnp.sum(edge + middle, axis=-1, keepdims=True)
        out = dot_nn(middle.astype(BF16), v_ref[pl.ds(at + TILE, TILE), lanes])
        out += dot_nn(jnp.where(recent, edge, 0.0).astype(BF16), v_ref[pl.ds(at + 2 * TILE, TILE), lanes])
        out += dot_nn(jnp.where(recent, 0.0, edge).astype(BF16), v_ref[pl.ds(at, TILE), lanes])
        att_ref[pl.ds(at, TILE), lanes] = out / total

    def attend_tile(tile, carry):
        for a in range(heads):
            attend(tile, a)
        return carry

    inner = WINDOW // TILE

    def attend_own():
        lax.fori_loop(inner, tiles, attend_tile, 0)

    def halo_ready():
        for copy in halo:
            copy.wait_recv()

    def update(old, step):
        moved = old + step
        before = jnp.sum(old * old, axis=-1, keepdims=True)
        after = jnp.sum(moved * moved, axis=-1, keepdims=True)
        return moved * (jnp.sqrt(before) / jnp.sqrt(after + EPSILON))

    def rows_of(position, part):
        return pl.ds(pl.multiple_of(lax.rem(position + 2 * NZ, NZ) * chunk + part * piece, piece), piece)

    own = pl.ds(pl.multiple_of(z * chunk, chunk), chunk)
    signs = (1, -1)
    ring = (z_next, z_prev)

    def gather_send(ref, ssem, rsem, index, part, way, step):
        block = ref.at[index, rows_of(z - signs[way] * step, part)]
        return remote(block, block, ssem.at[index, part, way, step], rsem.at[index, part, way, step], ring[way])

    def gather_take(ref, ssem, rsem, index, part, way, step):
        block = ref.at[index, rows_of(z - signs[way] * (step + 1), part)]
        return remote(block, block, ssem.at[index, part, way, step], rsem.at[index, part, way, step], ring[way])

    def gather_rest(ref, ssem, rsem, fill=None):
        for step in range(1, 5):
            for index, part in PIECES:
                for way in range(2):
                    if step <= hops_of(part, way):
                        gather_take(ref, ssem, rsem, index, part, way, step - 1).wait_recv()
                        if step < hops_of(part, way):
                            gather_send(ref, ssem, rsem, index, part, way, step).start()
                if fill is not None and (index, part) in PIECES[len(PIECES) // 2 - 1 :: len(PIECES) // 2]:
                    fill()

    def gather_drain(ref, ssem, rsem):
        for index, part in PIECES:
            for way in range(2):
                for step in range(hops_of(part, way)):
                    gather_send(ref, ssem, rsem, index, part, way, step).wait_send()

    def along_y(src, dst, ssem, rsem, target):
        return {(i, p): remote(src.at[i, p], dst.at[i, p], ssem.at[i, p], rsem.at[i, p], target) for i, p in PIECES}

    up_copies = along_y(ysend, up_recv, up_ssem, up_rsem, across)
    pair_copies = along_y(up_recv, up_pair, pair_ssem, pair_rsem, pair)
    y_copies = along_y(ysend, yrecv, y_ssem, y_rsem, pair)

    @pl.when(jnp.logical_and(upper, seq < last))
    def _():
        for copy in halo:
            copy.start()

    @pl.when(lower)
    def _():
        wa_ref[1] = w0t_ref[1].astype(BF16)
        wa_ref[2] = w0t_ref[2].astype(BF16)
        wdn_ref[...] = w0_ref[0].astype(BF16)
        for index in range(3):
            wc_ref[index] = w0t_ref[index, own, :]

    loads[6].wait()

    @pl.when(upper)
    def _():
        attend_own()
        for at in PIECES:
            up_copies[at].wait_recv()
            pair_copies[at].start()
        for index, part in PIECES:
            pair_copies[index, part].wait_recv()
            step = up_recv[index, part].astype(F32) + up_pair[index, part].astype(F32)
            fresh = update(w0t_ref[index, rows_of(z, part), :], step)
            wc_ref[index, pl.ds(part * piece, piece), :] = fresh
            wa_ref[index, rows_of(z, part), :] = fresh.astype(BF16)
            for way in range(2):
                gather_send(wa_ref, aga_ssem, aga_rsem, index, part, way, 0).start()
        gather_rest(wa_ref, aga_ssem, aga_rsem)
        gather_drain(wa_ref, aga_ssem, aga_rsem)
        for at in PIECES:
            pair_copies[at].wait_send()
        wdn_ref[...] = wa_ref[0].T

    def grad_tile(tile, carry):
        at = pl.multiple_of(tile * TILE, TILE)
        keys = kn_ref[pl.ds(at, TILE), :]
        gate_pre = dot_nt(wa_ref[1], keys)
        up_pre = dot_nt(wa_ref[2], keys)
        rate = rate_ref[0:1, pl.ds(at, TILE)].astype(F32)
        grad = dot_nt(wdn_ref[...], v_ref[pl.ds(at + WINDOW, TILE), :]) * rate
        sig = jax.nn.sigmoid(gate_pre)
        act = gate_pre * sig
        hid_ref[0, :, pl.ds(at, TILE)] = (act * up_pre * rate).astype(BF16)
        hid_ref[1, :, pl.ds(at, TILE)] = (grad * up_pre * sig * (1.0 + gate_pre * (1.0 - sig))).astype(BF16)
        hid_ref[2, :, pl.ds(at, TILE)] = (grad * act).astype(BF16)
        return carry

    lax.fori_loop(0, tiles, grad_tile, 0)

    def rs_copy(index, part, way, step):
        at = (index, part, way, step)
        return remote(rs_send.at[at], rs_recv.at[at], rs_ssem.at[at], rs_rsem.at[at], ring[way])

    def scatter_step(index, part, way, step):
        hops = hops_of(part, way)
        if step >= hops:
            return
        value = g_ref[index, rows_of(z + signs[way] * (hops - step), part), :]
        if step > 0:
            rs_copy(index, part, way, step - 1).wait_recv()
            value = value + rs_recv[index, part, way, step - 1].astype(F32)
        rs_send[index, part, way, step] = value.astype(BF16)
        rs_copy(index, part, way, step).start()

    def scatter_first(index):
        for part in range(SPLIT):
            for way in range(2):
                scatter_step(index, part, way, 0)

    g_ref[0] = dot_nn(hid_ref[0], v_ref[pl.ds(WINDOW, rows), :]).T
    scatter_first(0)
    g_ref[1] = dot_nn(hid_ref[1], kn_ref[...])
    scatter_first(1)
    g_ref[2] = dot_nn(hid_ref[2], kn_ref[...])
    scatter_first(2)
    for step in range(1, 4):
        for index, part in PIECES:
            for way in range(2):
                scatter_step(index, part, way, step)
    for index, part in PIECES:
        value = g_ref[index, rows_of(z, part), :]
        for way in range(2):
            final = hops_of(part, way) - 1
            rs_copy(index, part, way, final).wait_recv()
            value = value + rs_recv[index, part, way, final].astype(F32)
        ysend[index, part] = value.astype(BF16)
        y_copies[index, part].start()

        @pl.when(lower)
        def _():
            up_copies[index, part].start()

    for index, part in PIECES:
        y_copies[index, part].wait_recv()
        step = ysend[index, part].astype(F32) + yrecv[index, part].astype(F32)
        old = wc_ref[index, pl.ds(part * piece, piece), :]
        wb_ref[index, rows_of(z, part), :] = update(old, step).astype(BF16)
        for way in range(2):
            gather_send(wb_ref, agb_ssem, agb_rsem, index, part, way, 0).start()

    @pl.when(lower)
    def _():
        for at in PIECES:
            up_copies[at].wait_send()
        for copy in halo:
            copy.start()

    @pl.when(upper)
    def _():
        halo_ready()

    slots = [(tile, a) for tile in range(inner) for a in range(heads)]

    def fill():
        if slots:
            tile, a = slots.pop(0)

            @pl.when(upper)
            def _():
                attend(tile, a)

    gather_rest(wb_ref, agb_ssem, agb_rsem, fill)
    while slots:
        fill()

    @pl.when(lower)
    def _():
        attend_own()

        @pl.when(seq > 0)
        def _():
            halo_ready()

        lax.fori_loop(0, inner, attend_tile, 0)

    out_copies = []

    def apply_tile(tile, carry):
        at = pl.multiple_of(tile * TILE, TILE)
        queries = norm_rows(q_ref[pl.ds(at, TILE), :])
        gate_pre = dot_nt(queries, wb_ref[1])
        up_pre = dot_nt(queries, wb_ref[2])
        hidden = (gate_pre * jax.nn.sigmoid(gate_pre) * up_pre).astype(BF16)
        fast = dot_nt(hidden, wb_ref[0]).astype(BF16)
        out_ref[pl.ds(at, TILE), :] = (fast.astype(F32) + att_ref[pl.ds(at, TILE), :]).astype(BF16)
        pltpu.make_async_copy(
            out_ref.at[pl.ds(at, TILE)], out_hbm.at[pl.ds(at, TILE)], out_sem.at[tile]
        ).start()
        return carry

    lax.fori_loop(0, tiles, apply_tile, 0)

    gather_drain(wb_ref, agb_ssem, agb_rsem)
    for index, part in PIECES:
        for way in range(2):
            for step in range(hops_of(part, way)):
                rs_copy(index, part, way, step).wait_send()
        y_copies[index, part].wait_send()

    @pl.when(seq < last)
    def _():
        for copy in halo:
            copy.wait_send()

    for tile in range(tiles):
        at = tile * TILE
        pltpu.make_async_copy(
            out_ref.at[pl.ds(at, TILE)], out_hbm.at[pl.ds(at, TILE)], out_sem.at[tile]
        ).wait()


def on_device(queries, key_rows, value_rows, learn_rates, gate_fast, down_fast, up_fast):
    rows, width = queries.shape
    chunk = width // NZ
    tiles = rows // TILE
    dma = pltpu.SemaphoreType.DMA
    square = (3, width, width)
    piece = chunk // SPLIT
    parts = (3, SPLIT, 2, 4, piece, width)
    sems = (3, SPLIT, 2, 4)
    return pl.pallas_call(
        kernel,
        name="layer",
        out_shape=jax.ShapeDtypeStruct((rows, width), BF16),
        in_specs=[pl.BlockSpec(memory_space=pl.ANY)] * 7,
        out_specs=pl.BlockSpec(memory_space=pl.ANY),
        scratch_shapes=[
            pltpu.VMEM((rows, width), BF16),
            pltpu.VMEM((WINDOW + rows, width), BF16),
            pltpu.VMEM((WINDOW + rows, width), BF16),
            pltpu.VMEM((1, rows), BF16),
            pltpu.VMEM(square, F32),
            pltpu.VMEM(square, F32),
            pltpu.VMEM((rows, width), BF16),
            pltpu.VMEM(square, BF16),
            pltpu.VMEM(square[1:], BF16),
            pltpu.VMEM(square, BF16),
            pltpu.VMEM((3, chunk, width), F32),
            pltpu.VMEM((3, width, rows), BF16),
            pltpu.VMEM(square, F32),
            pltpu.VMEM(parts, BF16),
            pltpu.VMEM(parts, BF16),
            pltpu.VMEM((3, SPLIT, piece, width), BF16),
            pltpu.VMEM((3, SPLIT, piece, width), BF16),
            pltpu.VMEM((3, SPLIT, piece, width), BF16),
            pltpu.VMEM((3, SPLIT, piece, width), BF16),
            pltpu.VMEM((rows, width), F32),
            pltpu.VMEM((rows, width), BF16),
            dma((7,)),
            dma((tiles,)),
            dma((2,)),
            dma((2,)),
            dma(sems),
            dma(sems),
            dma((3, SPLIT)),
            dma((3, SPLIT)),
            dma((3, SPLIT)),
            dma((3, SPLIT)),
            dma((3, SPLIT)),
            dma((3, SPLIT)),
            dma(sems),
            dma(sems),
            dma(sems),
            dma(sems),
        ],
        compiler_params=pltpu.CompilerParams(
            collective_id=0, has_side_effects=True, vmem_limit_bytes=60 * 1024 * 1024
        ),
    )(queries, key_rows, value_rows, learn_rates.T, gate_fast, down_fast, up_fast)


def solution(mesh):
    return jax.shard_map(
        on_device,
        mesh=mesh,
        in_specs=(
            P("seq", "head"),
            P("seq", "head"),
            P("seq", "head"),
            P("seq", "head"),
            P("head", None, None),
            P("head", None, None),
            P("head", None, None),
        ),
        out_specs=P("seq", "head"),
        check_vma=False,
    )
```

time: 121 us -> 105 us (0.87)
  Pallas kernels: 119 us -> 102 us
    pallas_call x1, Pallas kernels: 119 us -> 102 us  [on_device(): pl.pallas_call(kernel, name='layer', out_shape=jax.ShapeDtypeStruct((rows...]
where the time goes in v2:
time: 105 us
  Pallas kernels  102 us (97%)
  local copies, waits for them, and re-layouts  2.65 us (3%)
    pallas_call x1, Pallas kernels, on_device(): pl.pallas_call(kernel, name='layer', out_shape=jax.ShapeDtypeStruct((rows...  102 us
    unnamed x1, local copies, waits for them, and re-layouts  2.65 us

profile of v2, /device:TPU:22, one launch (start us, length us, event | category | flops | bytes accessed | tf_op | source)
XLA Modules:
  0.0 104.7 jit_solution(17509703415050153885)
XLA Ops:
  0.0 102.0 %layer.1 = bf16[1536,512]{1,0:T(8,128)(2,1)} custom-call(bf16[1536,512]{1,0:T(8,128)(2,1)} %q_hbm.1, bf16[1536,512]{1,0:T(8,128)(2,1)} %k_hbm.1, bf16[1536,512]{1,0:T(8,128)(2,1)} %v_hbm.1, bf16[1,1536]{1,0:T(2,128)(2,1)} %bitcast.1, f32[1,512,512]{2,1,0:T(8,128)} %gate_hbm.1, f32[1,512,512]{2,1,0:T(8,128)} %down_hbm.1, f32[1,512,512]{2,1,0:T(8,128)} %up_hbm.1), custom_call_target="tpu_custom_call" | custom-call | tf_op jit(solution)/shard_map/layer/pallas_call | solution.py:397
  102.0 2.7 %copy.9 = bf16[1536,512]{1,0:T(8,128)(2,1)} copy(bf16[1536,512]{1,0:T(8,128)(2,1)} %layer.1) | data formatting | bytes 3145728

commit v3 on v2

v3 whole, which is shorter than its diff:
```python
import functools
import math

import jax
import jax.numpy as jnp
from jax import lax
from jax.experimental import pallas as pl
from jax.experimental.pallas import tpu as pltpu
from jax.sharding import PartitionSpec as P

AH = 128
WINDOW = 512
TILE = 256
NZ = 8
NY = 4
EPSILON = 1e-06
MESH = pl.DeviceIdType.MESH
HOPS = ((4, 3), (3, 4))
FAR = (1, 1)
F32 = jnp.float32
BF16 = jnp.bfloat16


def dot_nn(a, b):
    return lax.dot_general(a, b, (((1,), (0,)), ((), ())), preferred_element_type=F32)


def dot_nt(a, b):
    return lax.dot_general(a, b, (((1,), (1,)), ((), ())), preferred_element_type=F32)


def norm_rows(rows):
    as_float = rows.astype(F32)
    mean = jnp.mean(as_float * as_float, axis=-1, keepdims=True)
    return (as_float / jnp.sqrt(mean + EPSILON)).astype(BF16)


def kernel(
    q_hbm, k_hbm, v_hbm, rate_hbm, gate_hbm, down_hbm, up_hbm, out_ref,
    q_ref, k_ref, v_ref, rate_ref, w0_ref, w0t_ref, kn_ref, wa_ref, wdn_ref, wb_ref, wc_ref,
    hid_ref, g_ref, rs_send, rs_recv, xs_send, xs_recv, up_send, up_recv, att_ref,
    load_sem, halo_ssem, halo_rsem, rs_ssem, rs_rsem, xs_ssem, xs_rsem, up_ssem, up_rsem,
    aga_ssem, aga_rsem, xa_ssem, xa_rsem, agb_ssem, agb_rsem, xb_ssem, xb_rsem,
):
    rows, width = q_hbm.shape
    chunk = width // NZ
    piece = chunk // 2
    head = lax.axis_index("head")
    seq = lax.axis_index("seq")
    y = seq // NZ
    z = seq % NZ
    upper = y >= NY // 2
    lower = y < NY // 2
    last = NZ * NY - 1
    z_next = y * NZ + lax.rem(z + 1, NZ)
    z_prev = y * NZ + lax.rem(z + NZ - 1, NZ)
    pair = (y + 1 - 2 * lax.rem(y, 2)) * NZ + z
    across = (NY - 1 - y) * NZ + z
    heads = width // AH
    home = jnp.minimum(lax.rem(y, 3), 1)
    part_of = (home, 1 - home)
    tiles = rows // TILE

    def signal(target):
        pl.semaphore_signal(pltpu.get_barrier_semaphore(), inc=1, device_id=(head, target), device_id_type=MESH)

    def remote(src, dst, ssem, rsem, target):
        return pltpu.make_async_remote_copy(
            src_ref=src, dst_ref=dst, send_sem=ssem, recv_sem=rsem, device_id=(head, target), device_id_type=MESH
        )

    loads = [
        pltpu.make_async_copy(k_hbm, k_ref.at[pl.ds(WINDOW, rows)], load_sem.at[0]),
        pltpu.make_async_copy(gate_hbm.at[0], w0_ref.at[1], load_sem.at[1]),
        pltpu.make_async_copy(up_hbm.at[0], w0_ref.at[2], load_sem.at[2]),
        pltpu.make_async_copy(down_hbm.at[0], w0_ref.at[0], load_sem.at[3]),
        pltpu.make_async_copy(v_hbm, v_ref.at[pl.ds(WINDOW, rows)], load_sem.at[4]),
        pltpu.make_async_copy(rate_hbm, rate_ref, load_sem.at[5]),
        pltpu.make_async_copy(q_hbm, q_ref, load_sem.at[6]),
    ]
    for load in (loads[0], loads[1], loads[2], loads[4], loads[5], loads[3]):
        load.start()

    far_next = y * NZ + lax.rem(z + 2, NZ)
    far_prev = y * NZ + lax.rem(z + NZ - 2, NZ)
    for target in (z_next, z_prev, far_next, far_prev, pair, across):
        signal(target)
    edge_next = jnp.logical_and(z == NZ - 1, y < NY - 1)
    edge_prev = jnp.logical_and(z == 0, y > 0)

    @pl.when(edge_next)
    def _():
        signal(seq + 1)

    @pl.when(edge_prev)
    def _():
        signal(seq - 1)

    def norm_keys(tile, carry):
        at = pl.multiple_of(tile * TILE, TILE)
        kn_ref[pl.ds(at, TILE), :] = norm_rows(k_ref[pl.ds(at + WINDOW, TILE), :])
        return carry

    loads[0].wait()
    lax.fori_loop(0, tiles, norm_keys, 0)
    for index, load in ((1, loads[1]), (2, loads[2]), (0, loads[3])):
        load.wait()
        w0t_ref[index] = w0_ref[index].T
    loads[6].start()
    loads[4].wait()
    loads[5].wait()

    pl.semaphore_wait(
        pltpu.get_barrier_semaphore(), 6 + edge_next.astype(jnp.int32) + edge_prev.astype(jnp.int32)
    )

    halo = [
        remote(
            ref.at[pl.ds(rows, WINDOW)], ref.at[pl.ds(0, WINDOW)], halo_ssem.at[i], halo_rsem.at[i],
            lax.rem(seq + 1, NZ * NY),
        )
        for i, ref in enumerate((k_ref, v_ref))
    ]

    @pl.when(seq == 0)
    def _():
        k_ref[pl.ds(0, WINDOW), :] = jnp.zeros((WINDOW, width), BF16)
        v_ref[pl.ds(0, WINDOW), :] = jnp.zeros((WINDOW, width), BF16)

    def attend(tile, a):
        at = pl.multiple_of(tile * TILE, TILE)
        row = lax.broadcasted_iota(jnp.int32, (TILE, TILE), 0)
        col = lax.broadcasted_iota(jnp.int32, (TILE, TILE), 1)
        recent = col <= row
        real0 = jnp.logical_or(seq > 0, at >= WINDOW)
        real1 = jnp.logical_or(seq > 0, at + TILE >= WINDOW)
        scale = math.log2(math.e) / math.sqrt(AH)
        lanes = slice(a * AH, (a + 1) * AH)
        q = q_ref[pl.ds(at, TILE), lanes]
        s0 = dot_nt(q, k_ref[pl.ds(at, TILE), lanes])
        s1 = dot_nt(q, k_ref[pl.ds(at + TILE, TILE), lanes])
        s2 = dot_nt(q, k_ref[pl.ds(at + 2 * TILE, TILE), lanes])
        edge = jnp.where(recent, s2, jnp.where(real0, s0, -1e30))
        middle = jnp.where(real1, s1, -1e30)
        top = jnp.max(jnp.maximum(edge, middle), axis=-1, keepdims=True)
        edge = jnp.exp2((edge - top) * scale)
        middle = jnp.exp2((middle - top) * scale)
        total = jnp.sum(edge + middle, axis=-1, keepdims=True)
        out = dot_nn(middle.astype(BF16), v_ref[pl.ds(at + TILE, TILE), lanes])
        out += dot_nn(jnp.where(recent, edge, 0.0).astype(BF16), v_ref[pl.ds(at + 2 * TILE, TILE), lanes])
        out += dot_nn(jnp.where(recent, 0.0, edge).astype(BF16), v_ref[pl.ds(at, TILE), lanes])
        att_ref[pl.ds(at, TILE), lanes] = out / total

    def attend_tile(tile, carry):
        for a in range(heads):
            attend(tile, a)
        return carry

    inner = WINDOW // TILE

    def attend_own():
        lax.fori_loop(inner, tiles, attend_tile, 0)

    def halo_ready():
        for copy in halo:
            copy.wait_recv()

    def update(old, step):
        moved = old + step
        before = jnp.sum(old * old, axis=-1, keepdims=True)
        after = jnp.sum(moved * moved, axis=-1, keepdims=True)
        return moved * (jnp.sqrt(before) / jnp.sqrt(after + EPSILON))

    def rows_of(position, role):
        start = lax.rem(position + 2 * NZ, NZ) * chunk + part_of[role] * piece
        return pl.ds(pl.multiple_of(start, piece), piece)

    def sign_of(index, way):
        return 1 if (way + index) % 2 == 0 else -1

    def near(index, way):
        return z_next if sign_of(index, way) > 0 else z_prev

    def far(index, way):
        return far_next if sign_of(index, way) > 0 else far_prev

    def gather_copy(gather, index, role, way, step, distance, target):
        ref, ssem, rsem, _, _ = gather
        block = ref.at[index, rows_of(z - sign_of(index, way) * distance, role)]
        at = (index, role, way, step)
        return remote(block, block, ssem.at[at], rsem.at[at], target)

    def gather_send(gather, index, role, way, step):
        if (role, way) == FAR and step == 2:
            return gather_copy(gather, index, role, way, step, 2, far(index, way))
        return gather_copy(gather, index, role, way, step, step + role, near(index, way))

    def gather_take(gather, index, role, way, step):
        return gather_copy(gather, index, role, way, step, step + role + 1, near(index, way))

    def gather_cross(gather, index, kind, role):
        ref, _, _, ssem, rsem = gather
        distance = 0 if kind == 2 else sign_of(index, kind)
        block = ref.at[index, rows_of(z - distance, role)]
        return remote(block, block, ssem.at[index, kind], rsem.at[index, kind], pair)

    def gather_first(gather, index):
        for way in range(2):
            gather_send(gather, index, 0, way, 0).start()
        gather_cross(gather, index, 2, 0).start()

    def gather_rest(gather, fill=None):
        for hop in range(1, 5):
            for index in range(3):
                for way in range(2):
                    hops = HOPS[0][way]
                    if hop <= hops:
                        gather_take(gather, index, 0, way, hop - 1).wait_recv()
                        if hop == 1:
                            gather_cross(gather, index, way, 0).start()
                        if hop < hops:
                            gather_send(gather, index, 0, way, hop).start()
                for way in range(2):
                    if hop == 2:
                        gather_cross(gather, index, way, 1).wait_recv()
                        gather_send(gather, index, 1, way, 0).start()
                    if hop == 3:
                        gather_take(gather, index, 1, way, 0).wait_recv()
                        if (1, way) == FAR:
                            gather_send(gather, index, 1, way, 2).start()
                        gather_send(gather, index, 1, way, 1).start()
                    if hop == 4:
                        gather_take(gather, index, 1, way, 1).wait_recv()
                if hop == 2:
                    gather_cross(gather, index, 2, 1).wait_recv()
                if fill is not None:
                    fill()
        for index in range(3):
            gather_take(gather, index, *FAR, 2).wait_recv()

    def gather_drain(gather):
        for index in range(3):
            for way in range(2):
                for role in range(2):
                    for step in range(HOPS[role][way] - role):
                        gather_send(gather, index, role, way, step).wait_send()
            for kind in range(3):
                gather_cross(gather, index, kind, 0).wait_send()

    gather_a = (wa_ref, aga_ssem, aga_rsem, xa_ssem, xa_rsem)
    gather_b = (wb_ref, agb_ssem, agb_rsem, xb_ssem, xb_rsem)
    up_copies = [remote(up_send.at[i], up_recv.at[i], up_ssem.at[i], up_rsem.at[i], across) for i in range(3)]

    @pl.when(jnp.logical_and(upper, seq < last))
    def _():
        for copy in halo:
            copy.start()

    @pl.when(lower)
    def _():
        wa_ref[1] = w0t_ref[1].astype(BF16)
        wa_ref[2] = w0t_ref[2].astype(BF16)
        wdn_ref[...] = w0_ref[0].astype(BF16)
        for index in range(3):
            wc_ref[index] = w0t_ref[index, rows_of(z, 0), :]

    loads[6].wait()

    @pl.when(upper)
    def _():
        attend_own()
        for index in range(3):
            up_copies[index].wait_recv()
            fresh = update(w0t_ref[index, rows_of(z, 0), :], up_recv[index].astype(F32))
            wc_ref[index] = fresh
            wa_ref[index, rows_of(z, 0), :] = fresh.astype(BF16)
            gather_first(gather_a, index)
        gather_rest(gather_a)
        wdn_ref[...] = wa_ref[0].T

    def grad_tile(tile, carry):
        at = pl.multiple_of(tile * TILE, TILE)
        keys = kn_ref[pl.ds(at, TILE), :]
        gate_pre = dot_nt(wa_ref[1], keys)
        up_pre = dot_nt(wa_ref[2], keys)
        rate = rate_ref[0:1, pl.ds(at, TILE)].astype(F32)
        grad = dot_nt(wdn_ref[...], v_ref[pl.ds(at + WINDOW, TILE), :]) * rate
        sig = jax.nn.sigmoid(gate_pre)
        act = gate_pre * sig
        hid_ref[0, :, pl.ds(at, TILE)] = (act * up_pre * rate).astype(BF16)
        hid_ref[1, :, pl.ds(at, TILE)] = (grad * up_pre * sig * (1.0 + gate_pre * (1.0 - sig))).astype(BF16)
        hid_ref[2, :, pl.ds(at, TILE)] = (grad * act).astype(BF16)
        return carry

    lax.fori_loop(0, tiles, grad_tile, 0)

    def sum_copy(index, role, way, step):
        at = (index, role, way, step)
        target = far(index, way) if (role, way) == FAR and step == 0 else near(index, way)
        return remote(rs_send.at[at], rs_recv.at[at], rs_ssem.at[at], rs_rsem.at[at], target)

    def sum_cross(index, kind):
        at = (index, kind)
        return remote(xs_send.at[at], xs_recv.at[at], xs_ssem.at[at], xs_rsem.at[at], pair)

    def sum_step(index, role, way, step):
        hops = HOPS[role][way]
        value = g_ref[index, rows_of(z + sign_of(index, way) * (hops - step), role), :]
        before = [step - 1] if step > 0 else []
        if (role, way) == FAR:
            before = {2: [1, 0], 3: [2]}.get(step, [])
        for earlier in before:
            sum_copy(index, role, way, earlier).wait_recv()
            value = value + rs_recv[index, role, way, earlier].astype(F32)
        if step < hops - 1:
            rs_send[index, role, way, step] = value.astype(BF16)
            sum_copy(index, role, way, step).start()
        elif role == 1:
            xs_send[index, way] = value.astype(BF16)
            sum_cross(index, way).start()
        else:
            sum_cross(index, way).wait_recv()
            value = value + xs_recv[index, way].astype(F32)
            rs_send[index, role, way, step] = value.astype(BF16)
            sum_copy(index, role, way, step).start()

    def scatter_first(index):
        for role in (1, 0):
            for way in (1, 0):
                sum_step(index, role, way, 0)
        sum_step(index, *FAR, 1)
        xs_send[index, 2] = g_ref[index, rows_of(z, 1), :].astype(BF16)
        sum_cross(index, 2).start()

    g_ref[0] = dot_nn(hid_ref[0], v_ref[pl.ds(WINDOW, rows), :]).T
    scatter_first(0)
    g_ref[1] = dot_nn(hid_ref[1], kn_ref[...])
    scatter_first(1)
    g_ref[2] = dot_nn(hid_ref[2], kn_ref[...])
    scatter_first(2)
    for hop in range(1, 4):
        for index in range(3):
            if hop < 3:
                sum_step(index, 1, 0, hop)
            sum_step(index, 0, 0, hop)
            if hop == 1:
                sum_step(index, 0, 1, 1)
            if hop == 3:
                sum_step(index, 0, 1, 2)
        if hop < 3:
            for index in range(3):
                sum_step(index, 1, 1, hop + 1)
    for index in range(3):
        value = g_ref[index, rows_of(z, 0), :]
        sum_cross(index, 2).wait_recv()
        value = value + xs_recv[index, 2].astype(F32)
        for way in range(2):
            final = HOPS[0][way] - 1
            sum_copy(index, 0, way, final).wait_recv()
            value = value + rs_recv[index, 0, way, final].astype(F32)

        @pl.when(lower)
        def _():
            up_send[index] = value.astype(BF16)
            up_copies[index].start()

        wb_ref[index, rows_of(z, 0), :] = update(wc_ref[index], value).astype(BF16)
        gather_first(gather_b, index)

    @pl.when(lower)
    def _():
        for index in range(3):
            up_copies[index].wait_send()
        for copy in halo:
            copy.start()

    @pl.when(upper)
    def _():
        halo_ready()

    slots = [(tile, a) for tile in range(inner) for a in range(heads)]

    def fill():
        if slots:
            tile, a = slots.pop(0)

            @pl.when(upper)
            def _():
                attend(tile, a)

    gather_rest(gather_b, fill)
    while slots:
        fill()

    @pl.when(lower)
    def _():
        attend_own()

        @pl.when(seq > 0)
        def _():
            halo_ready()

        lax.fori_loop(0, inner, attend_tile, 0)

    out_copies = []

    def apply_tile(tile, carry):
        at = pl.multiple_of(tile * TILE, TILE)
        queries = norm_rows(q_ref[pl.ds(at, TILE), :])
        gate_pre = dot_nt(queries, wb_ref[1])
        up_pre = dot_nt(queries, wb_ref[2])
        hidden = (gate_pre * jax.nn.sigmoid(gate_pre) * up_pre).astype(BF16)
        fast = dot_nt(hidden, wb_ref[0]).astype(BF16)
        out_ref[pl.ds(at, TILE), :] = (fast.astype(F32) + att_ref[pl.ds(at, TILE), :]).astype(BF16)
        return carry

    lax.fori_loop(0, tiles, apply_tile, 0)

    gather_drain(gather_b)

    @pl.when(upper)
    def _():
        gather_drain(gather_a)

    for index in range(3):
        for way in range(2):
            for role in range(2):
                for step in range(HOPS[role][way] - role):
                    sum_copy(index, role, way, step).wait_send()
        for kind in range(3):
            sum_cross(index, kind).wait_send()

    @pl.when(seq < last)
    def _():
        for copy in halo:
            copy.wait_send()


def on_device(queries, key_rows, value_rows, learn_rates, gate_fast, down_fast, up_fast):
    rows, width = queries.shape
    chunk = width // NZ
    dma = pltpu.SemaphoreType.DMA
    square = (3, width, width)
    piece = chunk // 2
    sems = (3, 2, 2, 4)
    return pl.pallas_call(
        kernel,
        name="layer",
        out_shape=jax.ShapeDtypeStruct((rows, width), BF16),
        in_specs=[pl.BlockSpec(memory_space=pl.ANY)] * 7,
        out_specs=pl.BlockSpec(memory_space=pltpu.VMEM),
        scratch_shapes=[
            pltpu.VMEM((rows, width), BF16),
            pltpu.VMEM((WINDOW + rows, width), BF16),
            pltpu.VMEM((WINDOW + rows, width), BF16),
            pltpu.VMEM((1, rows), BF16),
            pltpu.VMEM(square, F32),
            pltpu.VMEM(square, F32),
            pltpu.VMEM((rows, width), BF16),
            pltpu.VMEM(square, BF16),
            pltpu.VMEM(square[1:], BF16),
            pltpu.VMEM(square, BF16),
            pltpu.VMEM((3, piece, width), F32),
            pltpu.VMEM((3, width, rows), BF16),
            pltpu.VMEM(square, F32),
            pltpu.VMEM(sems + (piece, width), BF16),
            pltpu.VMEM(sems + (piece, width), BF16),
            pltpu.VMEM((3, 3, piece, width), BF16),
            pltpu.VMEM((3, 3, piece, width), BF16),
            pltpu.VMEM((3, piece, width), BF16),
            pltpu.VMEM((3, piece, width), BF16),
            pltpu.VMEM((rows, width), F32),
            dma((7,)),
            dma((2,)),
            dma((2,)),
            dma(sems),
            dma(sems),
            dma((3, 3)),
            dma((3, 3)),
            dma((3,)),
            dma((3,)),
            dma(sems),
            dma(sems),
            dma((3, 3)),
            dma((3, 3)),
            dma(sems),
            dma(sems),
            dma((3, 3)),
            dma((3, 3)),
        ],
        compiler_params=pltpu.CompilerParams(
            collective_id=0, has_side_effects=True, vmem_limit_bytes=44 * 1024 * 1024
        ),
    )(
        *(
            pltpu.with_memory_space_constraint(array, pltpu.HBM)
            for array in (queries, key_rows, value_rows, learn_rates.T, gate_fast, down_fast, up_fast)
        )
    )


def solution(mesh):
    return jax.shard_map(
        on_device,
        mesh=mesh,
        in_specs=(
            P("seq", "head"),
            P("seq", "head"),
            P("seq", "head"),
            P("seq", "head"),
            P("head", None, None),
            P("head", None, None),
            P("head", None, None),
        ),
        out_specs=P("seq", "head"),
        check_vma=False,
    )
```

time: 105 us -> 103 us (0.981)
  local copies, waits for them, and re-layouts: 2.65 us -> 1.15 us
    unnamed x1, local copies, waits for them, and re-layouts: 2.65 us -> 1.15 us
where the time goes in v3:
time: 103 us
  Pallas kernels  102 us (99%)
  local copies, waits for them, and re-layouts  1.15 us (1%)
    pallas_call x1, Pallas kernels, on_device(): pl.pallas_call(kernel, name='layer', out_shape=jax.ShapeDtypeStruct((rows...  102 us

profile of v3, /device:TPU:22, one launch (start us, length us, event | category | flops | bytes accessed | tf_op | source)
XLA Modules:
  0.0 102.7 jit_solution(2290975941927844193)
XLA Ops:
  0.0 101.5 %layer.1 = bf16[1536,512]{1,0:T(8,128)(2,1)S(1)} custom-call(bf16[1536,512]{1,0:T(8,128)(2,1)} %q_hbm.1, bf16[1536,512]{1,0:T(8,128)(2,1)} %k_hbm.1, bf16[1536,512]{1,0:T(8,128)(2,1)} %v_hbm.1, bf16[1,1536]{1,0:T(2,128)(2,1)} %bitcast.1, f32[1,512,512]{2,1,0:T(8,128)} %gate_hbm.1, f32[1,512,512]{2,1,0:T(8,128)} %down_hbm.1, f32[1,512,512]{2,1,0:T(8,128)} %up_hbm.1), custom_call_target="tpu_custom_call" | custom-call | tf_op jit(solution)/shard_map/layer/pallas_call | solution.py:446
  101.5 1.1 %copy.9 = bf16[1536,512]{1,0:T(8,128)(2,1)} copy(bf16[1536,512]{1,0:T(8,128)(2,1)S(1)} %layer.1) | data formatting | bytes 3145728

commit v4 on v3

--- a/solution.py
+++ b/solution.py
@@ -103,9 +103,10 @@
 
     loads[0].wait()
     lax.fori_loop(0, tiles, norm_keys, 0)
-    for index, load in ((1, loads[1]), (2, loads[2]), (0, loads[3])):
+    for index, load in ((1, loads[1]), (2, loads[2])):
         load.wait()
         w0t_ref[index] = w0_ref[index].T
+    loads[3].wait()
     loads[6].start()
     loads[4].wait()
     loads[5].wait()
@@ -261,13 +262,11 @@
         wa_ref[1] = w0t_ref[1].astype(BF16)
         wa_ref[2] = w0t_ref[2].astype(BF16)
         wdn_ref[...] = w0_ref[0].astype(BF16)
-        for index in range(3):
-            wc_ref[index] = w0t_ref[index, rows_of(z, 0), :]
-
-    loads[6].wait()
 
     @pl.when(upper)
     def _():
+        w0t_ref[0] = w0_ref[0].T
+        loads[6].wait()
         attend_own()
         for index in range(3):
             up_copies[index].wait_recv()
@@ -338,6 +337,13 @@
     scatter_first(1)
     g_ref[2] = dot_nn(hid_ref[2], kn_ref[...])
     scatter_first(2)
+
+    @pl.when(lower)
+    def _():
+        w0t_ref[0] = w0_ref[0].T
+        for index in range(3):
+            wc_ref[index] = w0t_ref[index, rows_of(z, 0), :]
+
     for hop in range(1, 4):
         for index in range(3):
             if hop < 3:
@@ -394,6 +400,7 @@
 
     @pl.when(lower)
     def _():
+        loads[6].wait()
         attend_own()
 
         @pl.when(seq > 0)

time: 103 us -> 102 us (level)
  Pallas kernels: 102 us -> 100 us
    pallas_call x1, Pallas kernels: 102 us -> 100 us  [on_device(): pl.pallas_call(kernel, name='layer', out_shape=jax.ShapeDtypeStruct((rows...]
where the time goes in v4:
time: 102 us
  Pallas kernels  100 us (98%)
  local copies, waits for them, and re-layouts  1.15 us (1%)
    pallas_call x1, Pallas kernels, on_device(): pl.pallas_call(kernel, name='layer', out_shape=jax.ShapeDtypeStruct((rows...  100 us

profile of v4, /device:TPU:22, one launch (start us, length us, event | category | flops | bytes accessed | tf_op | source)
XLA Modules:
  0.0 101.6 jit_solution(12574741777491337343)
XLA Ops:
  0.0 100.4 %layer.1 = bf16[1536,512]{1,0:T(8,128)(2,1)S(1)} custom-call(bf16[1536,512]{1,0:T(8,128)(2,1)} %q_hbm.1, bf16[1536,512]{1,0:T(8,128)(2,1)} %k_hbm.1, bf16[1536,512]{1,0:T(8,128)(2,1)} %v_hbm.1, bf16[1,1536]{1,0:T(2,128)(2,1)} %bitcast.1, f32[1,512,512]{2,1,0:T(8,128)} %gate_hbm.1, f32[1,512,512]{2,1,0:T(8,128)} %down_hbm.1, f32[1,512,512]{2,1,0:T(8,128)} %up_hbm.1), custom_call_target="tpu_custom_call" | custom-call | tf_op jit(solution)/shard_map/layer/pallas_call | solution.py:453
  100.4 1.1 %copy.9 = bf16[1536,512]{1,0:T(8,128)(2,1)} copy(bf16[1536,512]{1,0:T(8,128)(2,1)S(1)} %layer.1) | data formatting | bytes 3145728
